TPU v7x, 32 devices: a whole 2x2x4 slice. The times are simulated.
32 devices in a mesh: ma: 16 (over z, x, core), af: 2 (over y).
Axes of the slice: x: 2, y: 2, z: 4, core: 2. Of those that a mesh axis runs over, the one named last changes fastest.
Arguments:
- coeffs: bfloat16 [512, 128, 2049], P('ma', 'af'), parts along dimension 1, may hold values from -6 to 6
- legendre: bfloat16 [512, 256, 2049], P('ma'), may hold values from -0.1875 to 0.1875
- assign: int32 [512], P('ma'), may hold values from 0 to 511, each once
Outputs:
- fourier: float32 [512, 128, 1024], P('ma', 'af'), parts along dimension 1
There are 2 independent parts, one for each index of `af`. A program takes and returns all parts, laid end to end along the dimension named above; an argument that names none is the same for every part. Nothing has to cross between parts.
Inputs may be any that keep to these rules, and one draw needn't show every extreme that they name: Slot s carries the wavenumbers assign[s] and 2047 - assign[s]; every pair appears once.
All inputs are finite; a program needn't handle non-finite values.
Results may differ from a plain program's by a relative error of at most 0.0003.
Values sent between devices are 32-bit elements; how exact they have to be, the bound alone decides.
A program may use at most 128 MiB of HBM per device.

v0:
```python
import jax
import jax.numpy as jnp
from jax import lax
from jax.sharding import PartitionSpec as P

TRUNC = 2047


def synthesize(coeffs, legendre, pair_ids):
    slots = coeffs.shape[0]
    columns = coeffs.shape[1]
    width = coeffs.shape[2]
    entry = lax.broadcasted_iota(jnp.int32, (slots, width), 1)
    first_len = (TRUNC + 1 - pair_ids)[:, None]
    second = entry >= first_len
    degree_gap = jnp.where(second, entry - first_len, entry)
    odd_gap = degree_gap % 2 == 1
    zero_value = jnp.zeros((), coeffs.dtype)
    group_masks = jnp.stack(
        [
            jnp.logical_and(jnp.logical_not(second), jnp.logical_not(odd_gap)),
            jnp.logical_and(jnp.logical_not(second), odd_gap),
            jnp.logical_and(second, jnp.logical_not(odd_gap)),
            jnp.logical_and(second, odd_gap),
        ],
        axis=1,
    )
    masked = jnp.where(group_masks[:, :, None, :], coeffs[:, None, :, :], zero_value)
    masked = masked.reshape(slots, 4 * columns, width)
    partial_value = jnp.einsum("shk,sgk->hgs", legendre, masked, preferred_element_type=jnp.float32)
    lat_half = partial_value.shape[0]
    partial_value = partial_value.reshape(lat_half, 4, columns, slots)
    north_rows = jnp.stack(
        [partial_value[:, 0] + partial_value[:, 1], partial_value[:, 2] + partial_value[:, 3]],
        axis=-1,
    )
    south_rows = jnp.stack(
        [partial_value[:, 0] - partial_value[:, 1], partial_value[:, 2] - partial_value[:, 3]],
        axis=-1,
    )
    north_rows = north_rows.reshape(lat_half, columns, 2 * slots)
    south_rows = south_rows.reshape(lat_half, columns, 2 * slots)
    return jnp.concatenate([north_rows, south_rows[::-1]], axis=0)


def column_places(all_pairs, devices, slots, pieces):
    total = devices * 2 * slots
    half_slots = slots // pieces
    column = jnp.arange(total, dtype=jnp.int32)
    piece_index = column // (devices * 2 * half_slots)
    within_piece = column % (devices * 2 * half_slots)
    source_device = within_piece // (2 * half_slots)
    within = within_piece % (2 * half_slots)
    global_slot = source_device * slots + piece_index * half_slots + within // 2
    owner_pair = jnp.take(all_pairs, global_slot)
    return jnp.where(within % 2 == 0, owner_pair, total - 1 - owner_pair)


def shards(coeffs, legendre, assign):
    devices = lax.axis_size("ma")
    slots = coeffs.shape[0]
    all_pairs = lax.all_gather(assign, "ma", axis=0, tiled=True)
    pieces = 1
    full_rows = synthesize(coeffs, legendre, assign)
    received = lax.all_to_all(full_rows, "ma", split_axis=0, concat_axis=2, tiled=True)
    column_place = column_places(all_pairs, devices, slots, pieces)
    total = received.shape[2]
    source_column = (
        jnp.zeros((total,), jnp.int32).at[column_place].set(jnp.arange(total, dtype=jnp.int32))
    )
    return jnp.take(received, source_column, axis=2)


def solution(mesh):
    return jax.shard_map(
        shards,
        mesh=mesh,
        in_specs=(P("ma", "af", None), P("ma", None, None), P("ma")),
        out_specs=P("ma", "af", None),
        check_vma=False,
    )
```

profile of v0, /device:TPU:15, one launch (start us, length us, event | category | flops | bytes accessed | tf_op | source)
XLA Modules:
  0.0 407.0 jit_solution(9538345013267640959)
XLA Ops:
  0.0 0.7 broadcast_subtract_fusion
  0.7 2.4 not_and_fusion.1
  3.1 1.4 pad_add_fusion
  4.5 14.4 %broadcast_select_fusion = bf16[32,4,64,2049]{3,2,1,0:T(8,128)(2,1)} fusion(pred[32,4,2049]{2,1,0:T(4,128)(4,1)S(1)} %pad_add_fusion, bf16[32,64,2049]{2,1,0:T(8,128)(2,1)} %param.3), kind=kLoop, calls=%fused_computation.3 | loop fusion | flops 16785408 | bytes 42225792 | tf_op jit(solution)/shard_map/jit(_where)/select_n | solution.py:28
  18.9 28.2 %fusion = f32[32,256,256]{2,1,0:T(8,128)} fusion(bf16[32,256,2049]{2,1,0:T(8,128)(2,1)} %bitcast.56, bf16[32,256,2049]{1,0,2:T(8,128)(2,1)} %param.4), kind=kOutput, calls=%fused_computation.4 | convolution fusion | flops 8594128896 | bytes 75530240 | tf_op jit(solution)/shard_map/shk,sgk->hgs/dot_general | solution.py:30
  47.1 5.8 %add_bitcast_fusion.1 = (f32[256,64,32,1]{0,1,3,2:T(8,128)S(1)}, f32[256,64,32,1]{0,1,3,2:T(8,128)}, f32[256,64,32,1]{0,1,2,3:T(8,128)S(1)}, f32[256,64,32,1]{0,1,2,3:T(8,128)S(1)}) fusion(f32[256,4,64,32]{0,2,1,3:T(8,128)} %bitcast.59), kind=kLoop, calls=%fused_computation.17 | loop fusion | flops 2097152 | bytes 16777216 | tf_op jit(solution)/shard_map/add | solution.py:34
  53.0 0.3 pad_maximum_fusion.2
  53.2 2.3 copy.41
  55.5 7.3 %rev.3 = f32[256,64,64]{0,1,2:T(8,128)} reverse(f32[256,64,64]{0,1,2:T(8,128)} %bitcast.57), dimensions={0} | reverse | bytes 8388608 | tf_op jit(solution)/shard_map/rev | solution.py:43
  62.8 0.0 copy-start
  62.8 2.1 pad_maximum_fusion.1
  64.9 0.7 copy-done
  65.6 4.5 %pad_maximum_fusion = f32[512,64,64]{0,1,2:T(8,128)} fusion(f32[256,64,64]{0,1,2:T(8,128)S(1)} %copy-done, f32[256,64,64]{0,1,2:T(8,128)S(1)} %bitcast.58), kind=kLoop, calls=%fused_computation.7 | loop fusion | flops 2097152 | bytes 16777216 | tf_op jit(solution)/shard_map/concatenate | solution.py:43
  70.1 16.2 %copy.42 = f32[512,64,64]{1,2,0:T(8,128)} copy(f32[512,64,64]{0,1,2:T(8,128)} %pad_maximum_fusion) | data formatting | bytes 16777216 | tf_op jit(solution)/shard_map/concatenate | solution.py:43
  86.4 18.4 %reshape.569 = f32[16,1,131072]{2,1,0:T(1,128)} reshape(f32[512,64,64]{2,1,0:T(8,128)} %bitcast.53) | data formatting | bytes 16777216
  104.8 0.0 copy-start.2
  104.8 6.7 %all-to-all-start = ((f32[16,1,131072]{2,1,0:T(1,128)}), f32[16,1,131072]{2,1,0:T(1,128)}, u32[]{:S(2)}, u32[]{:S(2)}) async-start(f32[16,1,131072]{2,1,0:T(1,128)} %reshape.569), calls=%async_computation | async-start | bytes 16777216 | tf_op jit(solution)/shard_map/all_to_all | solution.py:65
  111.4 0.0 copy-done.2
  111.4 0.6 dynamic-slice
  112.6 0.0 copy-done.1
  112.6 0.2 dynamic-update-slice
  112.8 178.7 %all-reduce = s32[512]{0:T(512)S(1)} all-reduce(s32[512]{0:T(512)S(1)} %dynamic-update-slice), channel_id=1, replica_groups=mesh['ma'=16,'af'=2] {'ma'}, use_global_device_ids=true, to_apply=%add | all-reduce | flops 512 | bytes 4096
  291.6 6.9 %gather_fusion = s32[1024]{0:T(1024)S(1)} fusion(s32[512]{0:T(512)S(1)} %all-reduce, s32[1024]{0:T(1024)S(1)} %broadcast_clamp_fusion), kind=kCustom, calls=%fused_computation | custom fusion | bytes 12288 | tf_op jit(solution)/shard_map/jit(_take)/gather | solution.py:55
  298.6 4.3 %scatter_custom_fusion = s32[1024]{0:T(1024)S(1)} fusion(s32[1024]{0:T(1024)S(1)} %bitcast.62, s32[1024]{0:T(1024)S(1)} %iota.27, s32[]{:T(128)} %constant.100.clone.1), kind=kCustom, calls=%fused_computation.53 | custom fusion | bytes 4100 | tf_op jit(solution)/shard_map/scatter | solution.py:69
  302.9 0.0 all-to-all-done
  302.9 0.5 broadcast.784
  303.4 25.2 %reduce = f32[16,131072]{1,0:T(8,128)} reduce(f32[16,1,131072]{2,1,0:T(1,128)} %all-to-all-done, f32[]{:T(128)} %broadcast.784), dimensions={1}, to_apply=%all_to_all.13.reduce_sub_computation | reduce | bytes 16777220 | tf_op jit(solution)/shard_map/all_to_all | solution.py:65
  328.7 17.4 %reshape.570 = f32[512,64,64]{2,1,0:T(8,128)} reshape(f32[16,131072]{1,0:T(8,128)} %reduce) | data formatting | bytes 16777216
  346.0 17.7 %copy.49 = f32[32,64,16,64]{1,0,3,2:T(8,128)} copy(f32[32,64,16,64]{1,3,0,2:T(8,128)} %bitcast.54) | data formatting | bytes 16777216 | tf_op jit(solution)/shard_map/all_to_all | solution.py:65
  363.7 18.2 %gather_fusion.1 = f32[1024,32,64]{2,1,0:T(8,128)} fusion(f32[32,64,1024]{1,0,2:T(8,128)} %bitcast.55, s32[1024]{0:T(1024)S(1)} %fusion.6), kind=kCustom, calls=%fused_computation.1 | custom fusion | bytes 16781312 | tf_op jit(solution)/shard_map/jit(_take)/gather | solution.py:71
  381.9 12.3 %select_bitcast_fusion = f32[32,64,1024]{1,0,2:T(8,128)} fusion(f32[1024,32,64]{2,1,0:T(8,128)} %gather_fusion.1, pred[1024]{0:T(1024)(128)(4,1)S(1)} %compare_and_fusion), kind=kLoop, calls=%fused_computation.6 | loop fusion | flops 2097152 | bytes 16778240 | tf_op jit(solution)/shard_map/jit(_take)/select_n | solution.py:71
  394.2 12.7 %copy.46 = f32[32,64,1024]{2,1,0:T(8,128)} copy(f32[32,64,1024]{1,0,2:T(8,128)} %select_bitcast_fusion) | data formatting | bytes 16777216 | tf_op jit(solution)/shard_map/jit(_take)/select_n | solution.py:71
  (8 shorter events, 0.1 us)
Async XLA Ops:
  62.8 2.8 copy-start
  104.8 6.7 %copy-start.2 = (u32[32]{0:T(128)S(1)}, u32[32]{0:T(128)}, u32[]{:S(2)}) copy-start(u32[32]{0:T(128)} %constant.119) | copy-start | bytes 388
  104.8 7.8 %copy-start.1 = (s32[32]{0:T(128)S(1)}, s32[32]{0:T(128)}, u32[]{:S(2)}) copy-start(s32[32]{0:T(128)} %param.5) | copy-start | bytes 388
  104.8 198.1 %all-to-all-start = ((f32[16,1,131072]{2,1,0:T(1,128)}), f32[16,1,131072]{2,1,0:T(1,128)}, u32[]{:S(2)}, u32[]{:S(2)}) async-start(f32[16,1,131072]{2,1,0:T(1,128)} %reshape.569), calls=%async_computation | async-start | bytes 16777216 | tf_op jit(solution)/shard_map/all_to_all | solution.py:65
where the time goes:
time: 413 us; the launch traced here: 407 us
  blocking collectives  179 us (43%)
  local copies, waits for them, and re-layouts  123 us (30%)
  other arithmetic  69.3 us (17%)
  matrix products  28.2 us (7%)
  starting transfers between devices  6.66 us (2%)
    unnamed x1, blocking collectives  179 us
    unnamed x11, local copies, waits for them, and re-layouts  37.3 us
    dot_general x1, matrix products, synthesize(): jnp.einsum('shk,sgk->hgs', legendre, masked, preferred_element_type=jnp.f...  28.2 us
    all_to_all x1, other arithmetic, shards(): lax.all_to_all(full_rows, 'ma', split_axis=0, concat_axis=2, tiled=True)  25.2 us
    all_to_all x2, local copies, waits for them, and re-layouts, shards(): lax.all_to_all(full_rows, 'ma', split_axis=0, concat_axis=2, tiled=True)  18.2 us
    gather x1, local copies, waits for them, and re-layouts, shards(): return jnp.take(received, source_column, axis=2)  18.2 us
    concatenate x1, local copies, waits for them, and re-layouts, synthesize(): return jnp.concatenate([north_rows, south_rows[::-1]], axis=0)  16.2 us
    select_n x1, other arithmetic, synthesize(): jnp.where(group_masks[:, :, None, :], coeffs[:, None, :, :], zero_value)  14.4 us
  transfers between devices with their start and end apart: 1, of which 0 were waited for; matrix products, arithmetic and copies ran while one was open for 3% of the time, Pallas kernels for 0%

commit v1 on v0

v1 whole, which is shorter than its diff:
```python
import functools

import jax
import jax.numpy as jnp
from jax import lax
from jax.experimental import pallas as pl
from jax.experimental.pallas import tpu as pltpu
from jax.sharding import PartitionSpec as P

TRUNC = 2047
ROWS_PER_STEP = 4
PIECES = 4
FIRST_PIECES = 1
LAST_PIECES = 1


def group_kernel(pairs_ref, coeff_ref, out_ref, *, start):
    held, columns, width = coeff_ref.shape
    pack = 16
    for slot in range(held):
        pair = pairs_ref[start + pl.program_id(0) * held + slot]
        group_slot(TRUNC + 1 - pair, coeff_ref.at[slot], out_ref.at[slot], pack)


def group_slot(first_len, coeff_ref, out_ref, pack):
    columns, width = coeff_ref.shape
    entry = lax.broadcasted_iota(jnp.int32, (pack, width), 1)
    first = entry < first_len
    odd_gap = (jnp.where(first, entry, entry - first_len) & 1) == 1
    sign = jnp.where(odd_gap, -1.0, 1.0)
    scales = [
        jnp.where(first, 1.0, 0.0),
        jnp.where(first, 0.0, 1.0),
        jnp.where(first, sign, 0.0),
        jnp.where(first, 0.0, sign),
    ]
    scales = [scale.astype(out_ref.dtype) for scale in scales]
    for low in range(0, columns, pack):
        values = coeff_ref[low:low + pack, :]
        for index, scale in enumerate(scales):
            at = index * columns + low
            out_ref[at:at + pack, :] = values * scale


def group_rows(coeffs, assign, start, part):
    _, columns, width = coeffs.shape
    held = 2 if part % 2 == 0 and start % 2 == 0 else 1
    return pl.pallas_call(
        functools.partial(group_kernel, start=start),
        grid_spec=pltpu.PrefetchScalarGridSpec(
            num_scalar_prefetch=1,
            grid=(part // held,),
            in_specs=[pl.BlockSpec((held, columns, width), lambda i, p: (start // held + i, 0, 0))],
            out_specs=pl.BlockSpec((held, 4 * columns, width), lambda i, p: (i, 0, 0)),
        ),
        out_shape=jax.ShapeDtypeStruct((part, 4 * columns, width), coeffs.dtype),
        cost_estimate=pl.CostEstimate(flops=0, transcendentals=0, bytes_accessed=part * columns * width * 10),
        name="group_rows",
    )(assign, coeffs)


def band_kernel(own_ref, *refs, band):
    out_ref = refs[-1]
    bands = out_ref.shape[0]
    south = pl.program_id(0)
    at = 0
    for value_ref in refs[:-1]:
        for slot in range(value_ref.shape[0]):
            rows = value_ref[slot].T
            for index in range(bands):
                to = jnp.where(south == 1, bands - 1 - index, index)
                out_ref[to, :band, at, :] = rows[index * band:(index + 1) * band]
            at += 1
    if out_ref.shape[1] > band:
        own = jnp.broadcast_to(own_ref[...], (bands, 1, at, own_ref.shape[-1]))
        out_ref[:, band:] = own


def band_rows(values, own, devices, extra):
    _, lanes, lat_half = values[0].shape
    part = sum(value.shape[0] for value in values)
    lanes //= 2
    bands = devices // 2
    band = lat_half // bands
    return pl.pallas_call(
        functools.partial(band_kernel, band=band),
        grid=(2,),
        in_specs=[pl.BlockSpec((1, lanes), lambda i: (0, 0))]
        + [pl.BlockSpec((value.shape[0], lanes, lat_half), lambda i: (0, i, 0)) for value in values],
        out_specs=pl.BlockSpec((bands, band + extra, part, lanes), lambda i: (i, 0, 0, 0)),
        out_shape=jax.ShapeDtypeStruct((devices, band + extra, part, lanes), jnp.float32),
        cost_estimate=pl.CostEstimate(
            flops=0, transcendentals=0, bytes_accessed=part * lanes * lat_half * 16
        ),
        name="band_rows",
    )(own, *values)


def chunk_rows(coeffs, legendre, assign, own, pieces, devices, extra):
    values = []
    for start, part in pieces:
        groups = group_rows(coeffs, assign, start, part)
        functions = lax.optimization_barrier(legendre[start:start + part])
        value = jnp.einsum("sgk,shk->sgh", groups, functions, preferred_element_type=jnp.float32)
        value, coeffs, legendre = lax.optimization_barrier((value, coeffs, legendre))
        values.append(value)
    return band_rows(values, own, devices, extra)


def place_kernel(flip_ref, pairs_ref, *refs, held):
    out_ref, place = refs[-2:]
    value_refs = refs[:-3] if held else refs[:-2]
    devices, rows, _, lanes = value_refs[0].shape
    count, total = place.shape
    total //= 2
    columns = lanes // 2

    @pl.when(pl.program_id(0) == 0)
    def _():
        pairs = jnp.broadcast_to(pairs_ref[...], (count, total))
        lane = lax.broadcasted_iota(jnp.int32, (count, total), 1)
        place[:, :total] = (pairs == lane).astype(jnp.bfloat16)
        place[:, total:] = (total - 1 - pairs == lane).astype(jnp.bfloat16)

    def by_lane(row):
        tiles = [ref[:, row].reshape(devices * ref.shape[2], lanes).T for ref in value_refs]
        return tiles[0] if len(tiles) == 1 else jnp.concatenate(tiles, axis=1)

    flip = flip_ref[0]
    values = jnp.concatenate([by_lane(row)[None] for row in range(rows)], axis=0)
    for half in range(2):
        mine = values[:, half * columns:(half + 1) * columns].reshape(rows * columns, count)
        high = mine.astype(jnp.bfloat16)
        low = (mine - high.astype(jnp.float32)).astype(jnp.bfloat16)
        span = slice(half * total, (half + 1) * total)
        placed = jnp.dot(high, place[:, span], preferred_element_type=jnp.float32)
        placed += jnp.dot(low, place[:, span], preferred_element_type=jnp.float32)
        placed = placed.reshape(rows, columns, total)
        for row in range(rows):
            to = jnp.where(flip == 1, rows - 1 - row, row)
            block = placed[row]
            if held:
                block += refs[-3][to, :, span]
            out_ref[to, :, span] = block


def place_columns(received, pairs, flip, band, total, placed):
    devices, _, _, lanes = received[0].shape
    count = pairs.shape[0]
    held = placed is not None
    steps = band // ROWS_PER_STEP
    columns = lanes // 2
    out_spec = pl.BlockSpec(
        (ROWS_PER_STEP, columns, 2 * total),
        lambda i, f: (jnp.where(f[0] == 1, steps - 1 - i, i), 0, 0),
    )
    return pl.pallas_call(
        functools.partial(place_kernel, held=held),
        grid_spec=pltpu.PrefetchScalarGridSpec(
            num_scalar_prefetch=1,
            grid=(steps,),
            in_specs=[pl.BlockSpec((count, 1), lambda i, f: (0, 0))]
            + [
                pl.BlockSpec((devices, ROWS_PER_STEP, block.shape[2], lanes), lambda i, f: (0, i, 0, 0))
                for block in received
            ]
            + ([out_spec] if held else []),
            out_specs=out_spec,
            scratch_shapes=[pltpu.VMEM((count, 2 * total), jnp.bfloat16)],
        ),
        out_shape=jax.ShapeDtypeStruct((band, columns, 2 * total), jnp.float32),
        cost_estimate=pl.CostEstimate(
            flops=4 * band * columns * count * total, transcendentals=0, bytes_accessed=32 * band * columns * total
        ),
        name="place_columns",
    )(flip, pairs, *received, *([placed] if held else []))


def shards(coeffs, legendre, assign):
    devices = lax.axis_size("ma")
    slots, columns, _ = coeffs.shape
    band = 2 * legendre.shape[1] // devices
    piece = max(slots // PIECES, 1)
    starts = list(range(0, slots, piece))
    bounds = [0, FIRST_PIECES, len(starts) - LAST_PIECES, len(starts)]
    own = jnp.pad(assign.astype(jnp.float32), (0, 2 * columns - slots))[None, :]
    flip = (lax.axis_index("ma") >= devices // 2).astype(jnp.int32)[None]
    received = []
    parts = []
    for low, high in zip(bounds, bounds[1:]):
        extra = 1 if low == 0 else 0
        pieces = [(start, min(piece, slots - start)) for start in starts[low:high]]
        rows = chunk_rows(coeffs, legendre, assign, own, pieces, devices, extra)
        rows, coeffs, legendre = lax.optimization_barrier((rows, coeffs, legendre))
        received.append(lax.all_to_all(rows, "ma", 0, 0, tiled=True))
        parts.append(sum(part for _, part in pieces))
    all_pairs = received[0][:, band, 0, :slots].astype(jnp.int32)
    ends = [sum(parts[:n]) for n in range(len(parts) + 1)]
    pairs = [all_pairs[:, low:high].reshape(-1, 1) for low, high in zip(ends, ends[1:])]
    early = jnp.concatenate(pairs[:-1], axis=0)
    placed = place_columns(received[:-1], early, flip, band, devices * slots, None)
    return place_columns(received[-1:], pairs[-1], flip, band, devices * slots, placed)


def solution(mesh):
    return jax.shard_map(
        shards,
        mesh=mesh,
        in_specs=(P("ma", "af", None), P("ma", None, None), P("ma")),
        out_specs=P("ma", "af", None),
        check_vma=False,
    )
```

time: 413 us -> 240 us (0.58); the launches traced: 407 us -> 239 us
  blocking collectives: 179 us -> 0 us
  waiting for transfers between devices: 0.01 us -> 113 us
  local copies, waits for them, and re-layouts: 123 us -> 15.9 us
  other arithmetic: 69.3 us -> 0.67 us
  Pallas kernels: 0 us -> 63.4 us
  starting transfers between devices: 6.66 us -> 16.1 us
    unnamed x1 -> x0, blocking collectives: 179 us -> none
    all_to_all x1 -> x3, waiting for transfers between devices: 0.01 us -> 113 us  [shards(): received.append(lax.all_to_all(rows, 'ma', 0, 0, tiled=True))]
    pallas_call x0 -> x9, Pallas kernels: none -> 63.4 us  [the longest x4 25.8 us: group_rows(): pl.pallas_call(functools.partial(group_kernel, start=start), grid_spec=pl...]
    unnamed x11 -> x2, local copies, waits for them, and re-layouts: 37.3 us -> 0.01 us
    select_n x4 -> x0, other arithmetic: 26.8 us -> none  [the longest x1 14.4 us: synthesize(): jnp.where(group_masks[:, :, None, :], coeffs[:, None, :, :], zero_value)]
    all_to_all x1 -> x0, other arithmetic: 25.2 us -> none  [shards(): lax.all_to_all(full_rows, 'ma', split_axis=0, concat_axis=2, tiled=True)]
    gather x2 -> x0, local copies, waits for them, and re-layouts: 25 us -> none  [the longest x1 18.2 us: shards(): return jnp.take(received, source_column, axis=2)]
    all_to_all x2 -> x0, local copies, waits for them, and re-layouts: 18.2 us -> none  [shards(): lax.all_to_all(full_rows, 'ma', split_axis=0, concat_axis=2, tiled=True)]
  transfers between devices with their start and end apart: 1 -> 3, of which waited for: 0 -> 3; matrix products, arithmetic and copies ran while one was open for 3% -> 10% of each run, Pallas kernels for 0% -> 17%
where the time goes in v1:
time: 240 us; the launch traced here: 239 us
  waiting for transfers between devices  113 us (47%)
  Pallas kernels  63.4 us (26%)
  matrix products  30 us (12%)
  starting transfers between devices  16.1 us (7%)
  local copies, waits for them, and re-layouts  15.9 us (7%)
    all_to_all x3, waiting for transfers between devices, shards(): received.append(lax.all_to_all(rows, 'ma', 0, 0, tiled=True))  113 us
    dot_general x4, matrix products, chunk_rows(): jnp.einsum('sgk,shk->sgh', groups, functions, preferred_element_type=jnp....  30 us
    pallas_call x4, Pallas kernels, group_rows(): pl.pallas_call(functools.partial(group_kernel, start=start), grid_spec=pl...  25.8 us
    pallas_call x2, Pallas kernels, place_columns(): pl.pallas_call(functools.partial(place_kernel, held=held), grid_spec=pltp...  22.5 us
    all_to_all x3, starting transfers between devices, shards(): received.append(lax.all_to_all(rows, 'ma', 0, 0, tiled=True))  16.1 us
    pallas_call x3, Pallas kernels, band_rows(): pl.pallas_call(functools.partial(band_kernel, band=band), grid=(2,), in_s...  15 us
    slice x8, local copies, waits for them, and re-layouts, chunk_rows(): functions = lax.optimization_barrier(legendre[start:start + part])  13.5 us
  transfers between devices with their start and end apart: 3, of which 3 were waited for; matrix products, arithmetic and copies ran while one was open for 10% of the time, Pallas kernels for 17%

profile of v1, /device:TPU:15, one launch (start us, length us, event | category | flops | bytes accessed | tf_op | source)
XLA Modules:
  0.0 238.6 jit_solution(9625184792470976488)
XLA Ops:
  0.0 0.7 convert_element_type.12
  0.7 0.5 pad_bitcast_fusion.own_ref
  1.1 6.5 %group_rows.4 = bf16[8,256,2049]{2,1,0:T(8,128)(2,1)} custom-call(s32[32]{0:T(128)} %pairs_ref.7, bf16[32,64,2049]{2,1,0:T(8,128)(2,1)} %coeff_ref.4), custom_call_target="tpu_custom_call" | custom-call | bytes 10490880 | tf_op jit(solution)/shard_map/group_rows/pallas_call | solution.py:48
  7.6 3.4 %slice-done = bf16[8,256,2049]{1,0,2:T(8,128)(2,1)S(1)} async-done(((bf16[32,256,2049]{1,0,2:T(8,128)(2,1)}), bf16[8,256,2049]{1,0,2:T(8,128)(2,1)S(1)}, s32[]{:S(2)}) %slice-start) | async-done | bytes 8392728 | tf_op jit(solution)/shard_map/slice | solution.py:103
  11.0 7.5 %fusion.6.refs_0_ = f32[8,256,256]{2,1,0:T(8,128)} fusion(bf16[8,256,2049]{2,1,0:T(8,128)(2,1)} %group_rows.4, bf16[8,256,2049]{1,0,2:T(8,128)(2,1)S(1)} %slice-done), kind=kOutput, calls=%fused_computation.6 | convolution fusion | flops 2148532224 | bytes 18882560 | tf_op jit(solution)/shard_map/sgk,shk->sgh/dot_general | solution.py:104
  18.5 4.2 %band_rows.3 = f32[16,33,8,128]{3,2,1,0:T(8,128)} custom-call(f32[1,128]{1,0:T(1,128)} %pad_bitcast_fusion.own_ref, f32[8,256,256]{2,1,0:T(8,128)} %fusion.6.refs_0_), custom_call_target="tpu_custom_call" | custom-call | bytes 4194304 | tf_op jit(solution)/shard_map/band_rows/pallas_call | solution.py:85
  22.6 6.5 %all-to-all-start = ((f32[16,33,8,128]{3,2,1,0:T(8,128)}), f32[16,33,8,128]{3,2,1,0:T(8,128)S(1)}, u32[]{:S(2)}, u32[]{:S(2)}) async-start(f32[16,33,8,128]{3,2,1,0:T(8,128)} %band_rows.3), calls=%async_computation | async-start | bytes 4325376 | tf_op jit(solution)/shard_map/all_to_all | solution.py:195
  29.2 6.5 %group_rows.5 = bf16[8,256,2049]{2,1,0:T(8,128)(2,1)} custom-call(s32[32]{0:T(128)} %pairs_ref.7, bf16[32,64,2049]{2,1,0:T(8,128)(2,1)} %coeff_ref.4), custom_call_target="tpu_custom_call" | custom-call | bytes 10490880 | tf_op jit(solution)/shard_map/group_rows/pallas_call | solution.py:48
  35.6 3.4 %slice-done.1 = bf16[8,256,2049]{1,0,2:T(8,128)(2,1)S(1)} async-done(((bf16[32,256,2049]{1,0,2:T(8,128)(2,1)}), bf16[8,256,2049]{1,0,2:T(8,128)(2,1)S(1)}, s32[]{:S(2)}) %slice-start.1) | async-done | bytes 8392728 | tf_op jit(solution)/shard_map/slice | solution.py:103
  39.0 7.6 %fusion.4.refs_0_ = f32[8,256,256]{2,1,0:T(8,128)} fusion(bf16[8,256,2049]{2,1,0:T(8,128)(2,1)} %group_rows.5, bf16[8,256,2049]{1,0,2:T(8,128)(2,1)S(1)} %slice-done.1), kind=kOutput, calls=%fused_computation.4 | convolution fusion | flops 2148532224 | bytes 18882560 | tf_op jit(solution)/shard_map/sgk,shk->sgh/dot_general | solution.py:104
  46.6 6.5 %group_rows.6 = bf16[8,256,2049]{2,1,0:T(8,128)(2,1)} custom-call(s32[32]{0:T(128)} %pairs_ref.7, bf16[32,64,2049]{2,1,0:T(8,128)(2,1)} %coeff_ref.4), custom_call_target="tpu_custom_call" | custom-call | bytes 10490880 | tf_op jit(solution)/shard_map/group_rows/pallas_call | solution.py:48
  53.0 3.4 %slice-done.2 = bf16[8,256,2049]{1,0,2:T(8,128)(2,1)S(1)} async-done(((bf16[32,256,2049]{1,0,2:T(8,128)(2,1)}), bf16[8,256,2049]{1,0,2:T(8,128)(2,1)S(1)}, s32[]{:S(2)}) %slice-start.2) | async-done | bytes 8392728 | tf_op jit(solution)/shard_map/slice | solution.py:103
  56.4 7.5 %fusion.2.refs_1_ = f32[8,256,256]{2,1,0:T(8,128)} fusion(bf16[8,256,2049]{2,1,0:T(8,128)(2,1)} %group_rows.6, bf16[8,256,2049]{1,0,2:T(8,128)(2,1)S(1)} %slice-done.2), kind=kOutput, calls=%fused_computation.2 | convolution fusion | flops 2148532224 | bytes 18882560 | tf_op jit(solution)/shard_map/sgk,shk->sgh/dot_general | solution.py:104
  63.9 6.7 %band_rows.4 = f32[16,32,16,128]{3,2,1,0:T(8,128)} custom-call(f32[1,128]{1,0:T(1,128)} %pad_bitcast_fusion.own_ref, f32[8,256,256]{2,1,0:T(8,128)} %fusion.4.refs_0_, f32[8,256,256]{2,1,0:T(8,128)} %fusion.2.refs_1_), custom_call_target="tpu_custom_call" | custom-call | bytes 8388608 | tf_op jit(solution)/shard_map/band_rows/pallas_call | solution.py:85
  70.6 7.4 %all-to-all-done.refs_0_ = f32[16,33,8,128]{3,2,1,0:T(8,128)S(1)} async-done(((f32[16,33,8,128]{3,2,1,0:T(8,128)}), f32[16,33,8,128]{3,2,1,0:T(8,128)S(1)}, u32[]{:S(2)}, u32[]{:S(2)}) %all-to-all-start) | async-done | bytes 2162720 | tf_op jit(solution)/shard_map/all_to_all | solution.py:195
  78.0 4.8 %all-to-all-start.2 = ((f32[16,32,16,128]{3,2,1,0:T(8,128)}), f32[16,32,16,128]{3,2,1,0:T(8,128)}, u32[]{:S(2)}, u32[]{:S(2)}) async-start(f32[16,32,16,128]{3,2,1,0:T(8,128)} %band_rows.4), calls=%async_computation.2 | async-start | bytes 8388608 | tf_op jit(solution)/shard_map/all_to_all | solution.py:195
  82.8 6.5 %group_rows.7 = bf16[8,256,2049]{2,1,0:T(8,128)(2,1)} custom-call(s32[32]{0:T(128)} %pairs_ref.7, bf16[32,64,2049]{2,1,0:T(8,128)(2,1)} %coeff_ref.4), custom_call_target="tpu_custom_call" | custom-call | bytes 10490880 | tf_op jit(solution)/shard_map/group_rows/pallas_call | solution.py:48
  89.2 3.4 %slice-done.3 = bf16[8,256,2049]{1,0,2:T(8,128)(2,1)S(1)} async-done(((bf16[32,256,2049]{1,0,2:T(8,128)(2,1)}), bf16[8,256,2049]{1,0,2:T(8,128)(2,1)S(1)}, s32[]{:S(2)}) %slice-start.3) | async-done | bytes 8392728 | tf_op jit(solution)/shard_map/slice | solution.py:103
  92.6 7.5 %fusion.refs_0_ = f32[8,256,256]{2,1,0:T(8,128)} fusion(bf16[8,256,2049]{2,1,0:T(8,128)(2,1)} %group_rows.7, bf16[8,256,2049]{1,0,2:T(8,128)(2,1)S(1)} %slice-done.3), kind=kOutput, calls=%fused_computation | convolution fusion | flops 2148532224 | bytes 18882560 | tf_op jit(solution)/shard_map/sgk,shk->sgh/dot_general | solution.py:104
  100.1 4.2 %band_rows.5 = f32[16,32,8,128]{3,2,1,0:T(8,128)} custom-call(f32[1,128]{1,0:T(1,128)} %pad_bitcast_fusion.own_ref, f32[8,256,256]{2,1,0:T(8,128)} %fusion.refs_0_), custom_call_target="tpu_custom_call" | custom-call | bytes 4194304 | tf_op jit(solution)/shard_map/band_rows/pallas_call | solution.py:85
  104.3 71.0 %all-to-all-done.2.refs_1_ = f32[16,32,16,128]{3,2,1,0:T(8,128)} async-done(((f32[16,32,16,128]{3,2,1,0:T(8,128)}), f32[16,32,16,128]{3,2,1,0:T(8,128)}, u32[]{:S(2)}, u32[]{:S(2)}) %all-to-all-start.2) | async-done | bytes 4194336 | tf_op jit(solution)/shard_map/all_to_all | solution.py:195
  175.2 4.8 %all-to-all-start.1 = ((f32[16,32,8,128]{3,2,1,0:T(8,128)}), f32[16,32,8,128]{3,2,1,0:T(8,128)}, u32[]{:S(2)}, u32[]{:S(2)}) async-start(f32[16,32,8,128]{3,2,1,0:T(8,128)} %band_rows.5), calls=%async_computation.1 | async-start | bytes 4194304 | tf_op jit(solution)/shard_map/all_to_all | solution.py:195
  180.0 0.0 copy-done
  180.0 0.1 slice.35
  180.1 0.1 fusion.8
  180.2 0.7 reshape.14.pairs_ref
  180.9 0.1 reshape.12
  180.9 0.1 reshape.11
  181.1 0.8 copy.34.pairs_ref
  181.9 11.5 %place_columns.2.refs_1_ = f32[32,64,1024]{2,1,0:T(8,128)} custom-call(s32[1]{0:T(128)} %bitcast.flip_ref, s32[384,1]{1,0:T(8,128)} %copy.34.pairs_ref, f32[16,33,8,128]{3,2,1,0:T(8,128)} %copy-done, f32[16,32,16,128]{3,2,1,0:T(8,128)} %all-to-all-done.2.refs_1_), custom_call_target="tpu_custom_call" | custom-call | flops 1610612736 | bytes 33554432 | tf_op jit(solution)/shard_map/place_columns/pallas_call | solution.py:157
  193.4 34.2 %all-to-all-done.1.refs_0_ = f32[16,32,8,128]{3,2,1,0:T(8,128)} async-done(((f32[16,32,8,128]{3,2,1,0:T(8,128)}), f32[16,32,8,128]{3,2,1,0:T(8,128)}, u32[]{:S(2)}, u32[]{:S(2)}) %all-to-all-start.1) | async-done | bytes 2097184 | tf_op jit(solution)/shard_map/all_to_all | solution.py:195
  227.5 11.1 %place_columns.3 = f32[32,64,1024]{2,1,0:T(8,128)} custom-call(s32[1]{0:T(128)} %bitcast.flip_ref, s32[128,1]{1,0:T(8,128)} %reshape.14.pairs_ref, f32[16,32,8,128]{3,2,1,0:T(8,128)} %all-to-all-done.1.refs_0_, f32[32,64,1024]{2,1,0:T(8,128)} %place_columns.2.refs_1_), custom_call_target="tpu_custom_call" | custom-call | flops 536870912 | bytes 33554432 | tf_op jit(solution)/shard_map/place_columns/pallas_call | solution.py:157
  (7 shorter events, 0.0 us)
Async XLA Ops:
  7.6 3.4 %slice-start = ((bf16[32,256,2049]{1,0,2:T(8,128)(2,1)}), bf16[8,256,2049]{1,0,2:T(8,128)(2,1)S(1)}, s32[]{:S(2)}) async-start(bf16[32,256,2049]{1,0,2:T(8,128)(2,1)} %param.4), calls=%async_computation.3 | async-start | bytes 16785408 | tf_op jit(solution)/shard_map/slice | solution.py:103
  22.6 55.3 %all-to-all-start = ((f32[16,33,8,128]{3,2,1,0:T(8,128)}), f32[16,33,8,128]{3,2,1,0:T(8,128)S(1)}, u32[]{:S(2)}, u32[]{:S(2)}) async-start(f32[16,33,8,128]{3,2,1,0:T(8,128)} %band_rows.3), calls=%async_computation | async-start | bytes 4325376 | tf_op jit(solution)/shard_map/all_to_all | solution.py:195
  35.6 3.4 %slice-start.1 = ((bf16[32,256,2049]{1,0,2:T(8,128)(2,1)}), bf16[8,256,2049]{1,0,2:T(8,128)(2,1)S(1)}, s32[]{:S(2)}) async-start(bf16[32,256,2049]{1,0,2:T(8,128)(2,1)} %param.4), calls=%async_computation.4 | async-start | bytes 16785408 | tf_op jit(solution)/shard_map/slice | solution.py:103
  53.0 3.4 %slice-start.2 = ((bf16[32,256,2049]{1,0,2:T(8,128)(2,1)}), bf16[8,256,2049]{1,0,2:T(8,128)(2,1)S(1)}, s32[]{:S(2)}) async-start(bf16[32,256,2049]{1,0,2:T(8,128)(2,1)} %param.4), calls=%async_computation.5 | async-start | bytes 16785408 | tf_op jit(solution)/shard_map/slice | solution.py:103
  78.0 102.0 %copy-start = (f32[16,33,8,128]{3,2,1,0:T(8,128)}, f32[16,33,8,128]{3,2,1,0:T(8,128)S(1)}, u32[]{:S(2)}) copy-start(f32[16,33,8,128]{3,2,1,0:T(8,128)S(1)} %all-to-all-done.refs_0_) | copy-start | bytes 6488068
  78.0 97.2 %all-to-all-start.2 = ((f32[16,32,16,128]{3,2,1,0:T(8,128)}), f32[16,32,16,128]{3,2,1,0:T(8,128)}, u32[]{:S(2)}, u32[]{:S(2)}) async-start(f32[16,32,16,128]{3,2,1,0:T(8,128)} %band_rows.4), calls=%async_computation.2 | async-start | bytes 8388608 | tf_op jit(solution)/shard_map/all_to_all | solution.py:195
  89.2 3.4 %slice-start.3 = ((bf16[32,256,2049]{1,0,2:T(8,128)(2,1)}), bf16[8,256,2049]{1,0,2:T(8,128)(2,1)S(1)}, s32[]{:S(2)}) async-start(bf16[32,256,2049]{1,0,2:T(8,128)(2,1)} %param.4), calls=%async_computation.6 | async-start | bytes 16785408 | tf_op jit(solution)/shard_map/slice | solution.py:103
  175.2 52.3 %all-to-all-start.1 = ((f32[16,32,8,128]{3,2,1,0:T(8,128)}), f32[16,32,8,128]{3,2,1,0:T(8,128)}, u32[]{:S(2)}, u32[]{:S(2)}) async-start(f32[16,32,8,128]{3,2,1,0:T(8,128)} %band_rows.5), calls=%async_computation.1 | async-start | bytes 4194304 | tf_op jit(solution)/shard_map/all_to_all | solution.py:195
